TPU v7x, 32 devices: a whole 2x2x4 slice. The times are simulated.
32 devices in a mesh: pair: 4 (over x, core), ep: 8 (over z, y).
Axes of the slice: x: 2, y: 2, z: 4, core: 2. Of those that a mesh axis runs over, the one named last changes fastest.
Arguments:
- tokens: bfloat16 [8192, 4096], P(('pair', 'ep')), may hold values from -6 to 6
- expert_of: int32 [8192, 1], P(('pair', 'ep')), may hold values from 0 to 31, as said below
- w_gate: bfloat16 [32, 4096, 768], P(('pair', 'ep')), may hold values from -0.09375 to 0.09375
- w_up: bfloat16 [32, 4096, 768], P(('pair', 'ep')), may hold values from -0.09375 to 0.09375
- w_down: bfloat16 [32, 768, 4096], P(('pair', 'ep')), may hold values from -0.21875 to 0.21875
Outputs:
- mixed: bfloat16 [8192, 4096], P(('pair', 'ep'))
Inputs may be any that keep to these rules, and one draw needn't show every extreme that they name: `expert_of`: the rows of one device (aligned blocks of 256 tokens) name no expert more than 12 times; in every draw one expert, drawn from the seed, is named exactly 12 times in every device's rows.
All inputs are finite; a program needn't handle non-finite values.
Results may differ from a plain program's by a relative error of at most 0.005.
Values may be sent and summed in bfloat16 or wider, within the bound.
A program may use at most 128 MiB of HBM per device.

v0:
```python
import jax
import jax.numpy as jnp
from jax import lax
from jax.sharding import PartitionSpec as P


def shards(tokens, expert_of, w_gate, w_up, w_down):
    pair_count = lax.axis_size("pair")
    ep_count = lax.axis_size("ep")
    experts = pair_count * ep_count
    tok_rows = tokens.shape[0]
    capacity = tok_rows // experts + tok_rows // (2 * experts)
    routed = expert_of[:, 0]
    onehot = (routed[:, None] == jnp.arange(experts, dtype=jnp.int32)[None, :]).astype(jnp.float32)
    earlier_mask = (jnp.arange(tok_rows)[:, None] > jnp.arange(tok_rows)[None, :]).astype(
        jnp.float32
    )
    before = jnp.dot(earlier_mask, onehot, precision=lax.Precision.HIGHEST)
    slot_index = jnp.sum(before * onehot, axis=1).astype(jnp.int32)
    position = routed * capacity + slot_index
    outgoing = (
        jnp.zeros((experts * capacity, tokens.shape[1]), jnp.bfloat16).at[position].set(tokens)
    )
    parcel = lax.all_to_all(
        outgoing.reshape(experts, capacity, outgoing.shape[1]),
        ("pair", "ep"),
        split_axis=0,
        concat_axis=0,
        tiled=True,
    )
    senders = parcel.shape[0]
    per_sender = parcel.shape[1]
    flat_rows = parcel.reshape(senders * per_sender, parcel.shape[2])
    gate_proj = jnp.dot(flat_rows, w_gate[0], preferred_element_type=jnp.float32)
    up_proj = jnp.dot(flat_rows, w_up[0], preferred_element_type=jnp.float32)
    hidden = (jax.nn.silu(gate_proj) * up_proj).astype(jnp.bfloat16)
    result = jnp.dot(hidden, w_down[0], preferred_element_type=jnp.float32).astype(jnp.bfloat16)
    returned = lax.all_to_all(
        result.reshape(senders, per_sender, result.shape[1]),
        ("pair", "ep"),
        split_axis=0,
        concat_axis=0,
        tiled=True,
    )
    returned = returned.reshape(experts * capacity, returned.shape[2])
    return jnp.take(returned, position, axis=0)


def solution(mesh):
    in_specs = (
        P(("pair", "ep"), None),
        P(("pair", "ep"), None),
        P(("pair", "ep"), None, None),
        P(("pair", "ep"), None, None),
        P(("pair", "ep"), None, None),
    )
    out_specs = P(("pair", "ep"), None)
    return jax.shard_map(shards, mesh=mesh, in_specs=in_specs, out_specs=out_specs, check_vma=False)
```

profile of v0, /device:TPU:0, one launch (start us, length us, event | category | flops | bytes accessed | tf_op | source)
XLA Modules:
  0.0 251.0 jit_solution(13829483784386282358)
XLA Ops:
  0.0 1.0 fusion.17
  1.0 0.7 and_reduce_fusion
  1.7 5.5 %scatter_custom_fusion = bf16[384,4096]{1,0:T(8,128)(2,1)S(1)} fusion(s32[256]{0:T(256)S(1)} %bitcast.22, bf16[256,4096]{1,0:T(8,128)(2,1)} %param.5, bf16[]{:T(256)} %constant.25.clone.1), kind=kCustom, calls=%fused_computation.10 | custom fusion | bytes 3146240 | tf_op jit(solution)/shard_map/scatter | solution.py:22
  7.2 2.7 %reshape.25 = bf16[32,12,4096]{2,1,0:T(8,128)(2,1)} reshape(bf16[384,4096]{1,0:T(8,128)(2,1)S(1)} %scatter_custom_fusion) | data formatting | bytes 6291456 | tf_op jit(solution)/shard_map/reshape | solution.py:25
  9.9 102.3 %all_to_all.10 = bf16[32,12,4096]{2,1,0:T(8,128)(2,1)} all-to-all(bf16[32,12,4096]{2,1,0:T(8,128)(2,1)} %reshape.25), channel_id=1, replica_groups=mesh['pair'=4,'ep'=8] {'pair','ep'}, dimensions={0} | all-to-all | bytes 6291456 | tf_op jit(solution)/shard_map/all_to_all | solution.py:24
  112.2 4.0 %reshape.26 = bf16[384,4096]{1,0:T(8,128)(2,1)S(1)} reshape(bf16[32,12,4096]{2,1,0:T(8,128)(2,1)} %all_to_all.10) | data formatting | bytes 6291456 | tf_op jit(solution)/shard_map/reshape | solution.py:33
  116.2 6.4 %fusion.4 = f32[384,768]{1,0:T(8,128)} fusion(bf16[384,4096]{1,0:T(8,128)(2,1)S(1)} %reshape.26, bf16[1,4096,768]{2,1,0:T(8,128)(2,1)} %param.7), kind=kOutput, calls=%fused_computation.6 | convolution fusion | flops 2415919104 | bytes 10616832 | tf_op jit(solution)/shard_map/dot_general | solution.py:34
  122.6 13.3 %fusion.6 = bf16[384,4096]{1,0:T(8,128)(2,1)} fusion(bf16[1,768,4096]{2,1,0:T(8,128)(2,1)} %param.9, bf16[384,4096]{1,0:T(8,128)(2,1)S(1)} %reshape.26, bf16[1,4096,768]{2,1,0:T(8,128)(2,1)} %param.8, f32[384,768]{1,0:T(8,128)} %fusion.4), kind=kOutput, calls=%fused_computation.8 | convolution fusion | flops 4835180544 | bytes 20054016 | tf_op jit(solution)/shard_map/dot_general | solution.py:37
  135.9 5.5 %reshape.27 = bf16[32,12,4096]{2,1,0:T(8,128)(2,1)} reshape(bf16[384,4096]{1,0:T(8,128)(2,1)} %fusion.6) | data formatting | bytes 6291456 | tf_op jit(solution)/shard_map/reshape | solution.py:39
  141.4 3.6 %all-to-all-start.1 = ((bf16[32,12,4096]{2,1,0:T(8,128)(2,1)}), bf16[32,12,4096]{2,1,0:T(8,128)(2,1)}, u32[]{:S(2)}, u32[]{:S(2)}) async-start(bf16[32,12,4096]{2,1,0:T(8,128)(2,1)} %reshape.27), calls=%async_computation.1 | async-start | bytes 8388608 | tf_op jit(solution)/shard_map/all_to_all | solution.py:38
  145.0 95.7 %all-to-all-done.1 = bf16[32,12,4096]{2,1,0:T(8,128)(2,1)} async-done(((bf16[32,12,4096]{2,1,0:T(8,128)(2,1)}), bf16[32,12,4096]{2,1,0:T(8,128)(2,1)}, u32[]{:S(2)}, u32[]{:S(2)}) %all-to-all-start.1) | async-done | bytes 3145760 | tf_op jit(solution)/shard_map/all_to_all | solution.py:38
  240.7 4.0 %reshape.28 = bf16[384,4096]{1,0:T(8,128)(2,1)S(1)} reshape(bf16[32,12,4096]{2,1,0:T(8,128)(2,1)} %all-to-all-done.1) | data formatting | bytes 6291456 | tf_op jit(solution)/shard_map/reshape | solution.py:45
  244.7 3.2 %gather_fusion = bf16[256,4096]{1,0:T(8,128)(2,1)} fusion(bf16[384,4096]{1,0:T(8,128)(2,1)S(1)} %reshape.28, s32[1024]{0:T(1024)S(1)} %pad_clamp_fusion), kind=kCustom, calls=%fused_computation | custom fusion | bytes 4195328 | tf_op jit(solution)/shard_map/jit(_take)/gather | solution.py:46
  247.9 3.2 %broadcast_select_fusion = bf16[256,4096]{1,0:T(8,128)(2,1)} fusion(bf16[256,4096]{1,0:T(8,128)(2,1)} %gather_fusion, pred[256]{0:T(512)(128)(4,1)S(1)} %get-tuple-element.5), kind=kLoop, calls=%fused_computation.9 | loop fusion | flops 1048576 | bytes 4194560 | tf_op jit(solution)/shard_map/jit(_take)/select_n | solution.py:46
  (2 shorter events, 0.0 us)
Async XLA Ops:
  141.4 99.3 %all-to-all-start.1 = ((bf16[32,12,4096]{2,1,0:T(8,128)(2,1)}), bf16[32,12,4096]{2,1,0:T(8,128)(2,1)}, u32[]{:S(2)}, u32[]{:S(2)}) async-start(bf16[32,12,4096]{2,1,0:T(8,128)(2,1)} %reshape.27), calls=%async_computation.1 | async-start | bytes 8388608 | tf_op jit(solution)/shard_map/all_to_all | solution.py:38
where the time goes:
time: 252 us; the launch traced here: 251 us
  blocking collectives  102 us (40%)
  waiting for transfers between devices  95.7 us (38%)
  local copies, waits for them, and re-layouts  24.8 us (10%)
  matrix products  20.7 us (8%)
  other arithmetic  3.88 us (2%)
  starting transfers between devices  3.57 us (1%)
    all_to_all x1, blocking collectives, shards(): lax.all_to_all(outgoing.reshape(experts, capacity, outgoing.shape[1]), ('...  102 us
    all_to_all x1, waiting for transfers between devices, shards(): lax.all_to_all(result.reshape(senders, per_sender, result.shape[1]), ('pa...  95.7 us
    dot_general x1, matrix products, shards(): jnp.dot(hidden, w_down[0], preferred_element_type=jnp.float32)  13.3 us
    dot_general x1, matrix products, shards(): jnp.dot(flat_rows, w_gate[0], preferred_element_type=jnp.float32)  6.4 us
    reshape x1, local copies, waits for them, and re-layouts, shards(): result.reshape(senders, per_sender, result.shape[1])  5.5 us
    scatter x1, local copies, waits for them, and re-layouts, shards(): jnp.zeros((experts * capacity, tokens.shape[1]), jnp.bfloat16).at[position]  5.48 us
  transfers between devices with their start and end apart: 1, of which 1 were waited for; matrix products, arithmetic and copies ran while one was open for 0% of the time, Pallas kernels for 0%

commit v1 on v0

v1 whole, which is shorter than its diff:
```python
import functools

import jax
import jax.numpy as jnp
from jax import lax
from jax.experimental import pallas as pl
from jax.experimental.pallas import tpu as pltpu
from jax.sharding import PartitionSpec as P

MESH = pl.DeviceIdType.MESH
TILE = 16
GROUP = 8


def dot(a, b):
    return jnp.dot(a, b, preferred_element_type=jnp.float32)


def exchange_ffn(
    pairs, eps, cap, out_ref, gate_hbm, up_hbm, down_hbm, ret_ref,
    recv, result, gate, up, down, hidden, rest,
    w_sem, local_sem, send1, recv1, send2, recv2,
):
    n = pairs * eps
    pair, ep = lax.axis_index("pair"), lax.axis_index("ep")
    me = pair * eps + ep
    width = recv.shape[2]
    tail = rest.shape[1]
    parts = cap // (TILE - cap)
    spare = TILE - cap

    def shift(k):
        i = k // pairs
        de = (eps // 2 + ((i + 1) // 2) * (2 * ((i + 1) % 2) - 1) + eps) % eps
        return (k + 1) % pairs, de

    def target(k):
        dp, de = shift(k)
        return lax.rem(pair + dp, pairs), lax.rem(ep + de, eps)

    def origin(k):
        dp, de = shift(k)
        return lax.rem(pair + pairs - dp, pairs), lax.rem(ep + eps - de, eps)

    loads = [
        pltpu.make_async_copy(src.at[0], dst, w_sem.at[i])
        for i, (src, dst) in enumerate(((gate_hbm, gate), (up_hbm, up), (down_hbm, down)))
    ]
    for load in loads:
        load.start()
    own = pltpu.make_async_copy(out_ref.at[me], recv.at[n - 1], local_sem.at[0])
    own.start()

    barrier = pltpu.get_barrier_semaphore()

    @pl.loop(0, n - 1)
    def _(k):
        p, e = target(k)
        pl.semaphore_signal(barrier, inc=1, device_id=(p, e), device_id_type=MESH)

    pl.semaphore_wait(barrier, n - 1)

    def outbound(k):
        p, e = target(k)
        return pltpu.make_async_remote_copy(
            src_ref=out_ref.at[p * eps + e],
            dst_ref=recv.at[k],
            send_sem=send1.at[k],
            recv_sem=recv1.at[k],
            device_id=(p, e),
            device_id_type=MESH,
        )

    def inbound(k):
        p, e = origin(k)
        return pltpu.make_async_remote_copy(
            src_ref=result.at[k],
            dst_ref=ret_ref.at[me],
            send_sem=send2.at[k],
            recv_sem=recv2.at[me],
            device_id=(p, e),
            device_id_type=MESH,
        )

    @pl.loop(0, n - 1)
    def _(k):
        outbound(k).start()

    for load in loads:
        load.wait()
    own.wait()

    rows = GROUP * TILE
    r = lax.broadcasted_iota(jnp.int32, (rows, rows), 0)
    c = lax.broadcasted_iota(jnp.int32, (rows, rows), 1)
    same = (r // TILE) == (c // TILE)
    r, c = r % TILE, c % TILE

    def unpacker(j):
        pick = same & (r // spare == j) & (c == cap + r % spare)
        return pick.astype(jnp.float32).astype(jnp.bfloat16)

    def packer(j):
        pick = same & (r >= cap) & (c == spare * j + r - cap)
        return pick.astype(jnp.float32).astype(jnp.bfloat16)

    body_row = (lax.broadcasted_iota(jnp.int32, (rows, 1), 0) % TILE) < cap
    step = 256

    @pl.loop(0, n // GROUP)
    def _(g):
        first = g * GROUP

        @pl.loop(0, GROUP)
        def _(i):
            @pl.when(first + i < n - 1)
            def _():
                outbound(first + i).wait_recv()

        block = recv.at[pl.ds(first, GROUP)]
        total = jnp.zeros((rows, tail), jnp.float32)
        for j in range(parts):
            piece = block[:, :, j * tail:(j + 1) * tail].reshape(rows, tail)
            total = total + dot(unpacker(j), piece)
        rest[...] = total.astype(jnp.bfloat16)

        @pl.loop(0, hidden.shape[1] // step)
        def _(f):
            cols = pl.ds(pl.multiple_of(f * step, step), step)
            main = block[...].reshape(rows, width)
            g_out = dot(main, gate[:width, cols]) + dot(rest[...], gate[width:, cols])
            u_out = dot(main, up[:width, cols]) + dot(rest[...], up[width:, cols])
            hidden[:, cols] = (jax.nn.silu(g_out) * u_out).astype(jnp.bfloat16)

        rest[...] = dot(hidden[...], down[:, width:]).astype(jnp.bfloat16)
        for j in range(parts):
            cols = pl.ds(j * tail, tail)
            body = dot(hidden[...], down[:, cols])
            extra = dot(packer(j), rest[...])
            packed = jnp.where(body_row, body, extra).astype(jnp.bfloat16)
            result[pl.ds(first, GROUP), :, cols] = packed.reshape(GROUP, TILE, tail)

        @pl.loop(0, GROUP)
        def _(i):
            @pl.when(first + i < n - 1)
            def _():
                inbound(first + i).start()

    mine = pltpu.make_async_copy(result.at[n - 1], ret_ref.at[me], local_sem.at[1])
    mine.start()
    mine.wait()

    @pl.loop(0, n - 1)
    def _(k):
        outbound(k).wait_send()
        inbound(k).wait_send()
        p, e = target(k)
        peer = p * eps + e
        pltpu.make_async_remote_copy(
            src_ref=result.at[k],
            dst_ref=ret_ref.at[peer],
            send_sem=send2.at[k],
            recv_sem=recv2.at[peer],
            device_id=(p, e),
            device_id_type=MESH,
        ).wait_recv()


def fused(tokens, routed, slot, w_gate, w_up, w_down, pairs, eps, cap):
    n = pairs * eps
    tok_rows, depth = tokens.shape
    ff = w_gate.shape[2]
    spare = TILE - cap
    parts = cap // spare
    tail = depth * spare // TILE
    width = depth - tail

    row = jnp.arange(n * TILE, dtype=jnp.int32)
    key = routed * TILE + slot
    main_sel = key[:, None] == row[None, :]
    rest_key = jnp.where(
        slot[:, None] // spare == jnp.arange(parts)[None, :],
        (routed * TILE + cap + slot % spare)[:, None],
        -1,
    )
    rest_sel = [rest_key[:, j][:, None] == row[None, :] for j in range(parts)]
    main_f = main_sel.astype(jnp.bfloat16)
    rest_f = [s.astype(jnp.bfloat16) for s in rest_sel]
    last = tokens[:, width:]
    pieces = []
    for j in range(parts):
        both = jnp.concatenate([main_f, rest_f[j]], axis=0)
        rows = jnp.concatenate([tokens[:, j * tail:(j + 1) * tail], last], axis=0)
        pieces.append(
            lax.dot_general(
                both, rows, (((0,), (0,)), ((), ())), preferred_element_type=jnp.float32
            ).astype(jnp.bfloat16)
        )
    outgoing = jnp.concatenate(pieces, axis=1).reshape(n, TILE, width)

    vmem = pl.BlockSpec(memory_space=pltpu.VMEM)
    hbm = pl.BlockSpec(memory_space=pl.ANY)
    bf16 = jnp.bfloat16
    returned = pl.pallas_call(
        functools.partial(exchange_ffn, pairs, eps, cap),
        out_shape=jax.ShapeDtypeStruct((n, TILE, width), bf16),
        in_specs=[vmem, hbm, hbm, hbm],
        out_specs=vmem,
        scratch_shapes=[
            pltpu.VMEM((n, TILE, width), bf16),
            pltpu.VMEM((n, TILE, width), bf16),
            pltpu.VMEM((depth, ff), bf16),
            pltpu.VMEM((depth, ff), bf16),
            pltpu.VMEM((ff, depth), bf16),
            pltpu.VMEM((GROUP * TILE, ff), bf16),
            pltpu.VMEM((GROUP * TILE, tail), bf16),
            pltpu.SemaphoreType.DMA((3,)),
            pltpu.SemaphoreType.DMA((2,)),
            pltpu.SemaphoreType.DMA((n,)),
            pltpu.SemaphoreType.DMA((n,)),
            pltpu.SemaphoreType.DMA((n,)),
            pltpu.SemaphoreType.DMA((n,)),
        ],
        compiler_params=pltpu.CompilerParams(
            collective_id=0, has_side_effects=True, vmem_limit_bytes=56 * 1024 * 1024
        ),
        name="exchange_ffn",
    )(outgoing, w_gate, w_up, w_down)
    back = returned.reshape(n * TILE, width)
    head = dot(main_f, back).astype(bf16)
    ends = sum(dot(rest_f[j], back[:, j * tail:(j + 1) * tail]) for j in range(parts))
    return jnp.concatenate([head, ends.astype(bf16)], axis=1)


def plain(tokens, routed, slot, w_gate, w_up, w_down, experts, capacity):
    position = routed * capacity + slot
    outgoing = (
        jnp.zeros((experts * capacity, tokens.shape[1]), jnp.bfloat16).at[position].set(tokens)
    )
    parcel = lax.all_to_all(
        outgoing.reshape(experts, capacity, outgoing.shape[1]),
        ("pair", "ep"), split_axis=0, concat_axis=0, tiled=True,
    )
    flat_rows = parcel.reshape(experts * capacity, parcel.shape[2])
    gate_proj = dot(flat_rows, w_gate[0])
    up_proj = dot(flat_rows, w_up[0])
    hidden = (jax.nn.silu(gate_proj) * up_proj).astype(jnp.bfloat16)
    result = dot(hidden, w_down[0]).astype(jnp.bfloat16)
    returned = lax.all_to_all(
        result.reshape(experts, capacity, result.shape[1]),
        ("pair", "ep"), split_axis=0, concat_axis=0, tiled=True,
    )
    return jnp.take(returned.reshape(experts * capacity, -1), position, axis=0)


def shards(tokens, expert_of, w_gate, w_up, w_down):
    pairs = lax.axis_size("pair")
    eps = lax.axis_size("ep")
    experts = pairs * eps
    tok_rows, depth = tokens.shape
    cap = tok_rows // experts + tok_rows // (2 * experts)
    routed = expert_of[:, 0]
    onehot = (routed[:, None] == jnp.arange(experts, dtype=jnp.int32)[None, :]).astype(jnp.float32)
    order = jnp.arange(tok_rows)
    earlier = (order[:, None] > order[None, :]).astype(jnp.bfloat16)
    before = dot(earlier, onehot.astype(jnp.bfloat16))
    slot = jnp.sum(before * onehot, axis=1).astype(jnp.int32)
    spare = TILE - cap
    packs = 0 < spare <= cap and cap % spare == 0 and (depth * spare) % (TILE * 256) == 0
    if packs and experts % GROUP == 0 and w_gate.shape[2] % 256 == 0:
        return fused(tokens, routed, slot, w_gate, w_up, w_down, pairs, eps, cap)
    return plain(tokens, routed, slot, w_gate, w_up, w_down, experts, cap)


def solution(mesh):
    spec2 = P(("pair", "ep"), None)
    spec3 = P(("pair", "ep"), None, None)
    return jax.shard_map(
        shards,
        mesh=mesh,
        in_specs=(spec2, spec2, spec3, spec3, spec3),
        out_specs=spec2,
        check_vma=False,
    )
```

time: 252 us -> 165 us (0.65)
  the two profiles are of different devices: /device:TPU:0 before, /device:TPU:12 now
where the time goes in v1:
time: 165 us
  Pallas kernels  151 us (92%)
  matrix products  8.25 us (5%)
  other arithmetic  4.35 us (3%)
  local copies, waits for them, and re-layouts  1.75 us (1%)
    pallas_call x1, Pallas kernels, fused(): pl.pallas_call(functools.partial(exchange_ffn, pairs, eps, cap), out_shap...  151 us
    dot_general x5, matrix products, dot(): return jnp.dot(a, b, preferred_element_type=jnp.float32)  6.06 us

profile of v1, /device:TPU:12, one launch (start us, length us, event | category | flops | bytes accessed | tf_op | source)
XLA Modules:
  0.0 165.2 jit_solution(12449629282755954270)
XLA Ops:
  0.0 1.0 fusion.1
  1.0 0.7 fusion.22
  1.7 0.1 fusion.14
  1.8 0.1 fusion.13
  1.9 0.2 fusion.12
  2.1 1.7 %fusion.27 = (bf16[256,1024]{1,0:T(8,128)(2,1)S(1)}, bf16[256,1024]{1,0:T(8,128)(2,1)S(1)}, bf16[256,1024]{1,0:T(8,128)(2,1)S(1)}, bf16[256,1024]{1,0:T(8,128)(2,1)S(1)}) fusion(bf16[256,4096]{1,0:T(8,128)(2,1)} %param.5), kind=kLoop, calls=%fused_computation.58 | loop fusion | bytes 4194304 | tf_op jit(solution)/shard_map/slice | solution.py:193
  3.8 0.7 convolution_convert_fusion.3
  4.6 0.7 convolution_convert_fusion.1
  5.3 0.7 convolution_convert_fusion.2
  6.1 1.8 %pad_maximum_fusion = bf16[512,3072]{1,0:T(8,128)(2,1)} fusion(bf16[512,1024]{1,0:T(8,128)(2,1)S(1)} %convolution_convert_fusion.1, bf16[512,1024]{1,0:T(8,128)(2,1)S(1)} %convolution_convert_fusion.2, bf16[512,1024]{1,0:T(8,128)(2,1)S(1)} %convolution_convert_fusion.3), kind=kLoop, calls=%fused_computation.1 | loop fusion | flops 9437184 | bytes 6291456 | tf_op jit(solution)/shard_map/concatenate | solution.py:199
  7.8 150.7 %exchange_ffn.1 = bf16[32,16,3072]{2,1,0:T(8,128)(2,1)} custom-call(bf16[32,16,3072]{2,1,0:T(8,128)(2,1)} %bitcast.14, bf16[1,4096,768]{2,1,0:T(8,128)(2,1)} %gate_hbm.1, bf16[1,4096,768]{2,1,0:T(8,128)(2,1)} %up_hbm.1, bf16[1,768,4096]{2,1,0:T(8,128)(2,1)} %down_hbm.1), custom_call_target="tpu_custom_call" | custom-call | tf_op jit(solution)/shard_map/exchange_ffn/pallas_call | solution.py:204
  158.6 0.0 copy-start
  158.6 1.9 %fusion.4 = f32[256,1024]{1,0:T(8,128)S(1)} fusion(bf16[512,3072]{1,0:T(8,128)(2,1)} %bitcast.10, s32[256]{0:T(256)S(1)} %bitcast.22), kind=kOutput, calls=%fused_computation.16 | convolution fusion | flops 268566528 | bytes 2098176 | tf_op jit(solution)/shard_map/dot_general | solution.py:16
  160.5 1.7 %convolution_add_fusion.1 = f32[256,1024]{1,0:T(8,128)S(1)} fusion(f32[256,1024]{1,0:T(8,128)S(1)} %fusion.4, bf16[512,3072]{1,0:T(8,128)(2,1)} %bitcast.11, s32[256]{0:T(256)S(1)} %bitcast.20), kind=kOutput, calls=%fused_computation.7 | convolution fusion | flops 268828672 | bytes 3146752 | tf_op jit(solution)/shard_map/dot_general | solution.py:16
  162.2 0.0 copy-done
  162.2 0.5 fusion
  162.7 1.1 convolution_convert_fusion
  163.7 1.5 pad_maximum_fusion.1
  (4 shorter events, 0.0 us)
Async XLA Ops:
  158.6 3.6 %copy-start = (bf16[32,16,3072]{2,1,0:T(8,128)(2,1)S(1)}, bf16[32,16,3072]{2,1,0:T(8,128)(2,1)}, u32[]{:S(2)}) copy-start(bf16[32,16,3072]{2,1,0:T(8,128)(2,1)} %exchange_ffn.1) | copy-start | bytes 9437188

commit v2 on v1

v2 whole, which is shorter than its diff:
```python
import functools

import jax
import jax.numpy as jnp
from jax import lax
from jax.experimental import pallas as pl
from jax.experimental.pallas import tpu as pltpu
from jax.sharding import PartitionSpec as P

MESH = pl.DeviceIdType.MESH
TILE = 16
GROUP = 8


def dot(a, b):
    return jnp.dot(a, b, preferred_element_type=jnp.float32)


def exchange_ffn(
    pairs, eps, cap, row_keys, col_keys, tok_hbm, gate_hbm, up_hbm, down_hbm, mixed_ref,
    tok, outgoing, recv, result, returned, gate, up, down, hidden, rest,
    tok_sem, w_sem, local_sem, send1, recv1, send2, recv2,
):
    n = pairs * eps
    pair, ep = lax.axis_index("pair"), lax.axis_index("ep")
    tok_rows = tok.shape[0]
    width = recv.shape[2]
    tail = rest.shape[1]
    parts = cap // (TILE - cap)
    spare = TILE - cap
    rows = GROUP * TILE
    bf16 = jnp.bfloat16

    def shift(k):
        i = k // pairs
        de = (eps // 2 + ((i + 1) // 2) * (2 * ((i + 1) % 2) - 1) + eps) % eps
        return (k + 1) % pairs, de

    def target(k):
        dp, de = shift(k)
        return lax.rem(pair + dp, pairs), lax.rem(ep + de, eps)

    def origin(k):
        dp, de = shift(k)
        return lax.rem(pair + pairs - dp, pairs), lax.rem(ep + eps - de, eps)

    tok_load = pltpu.make_async_copy(tok_hbm, tok, tok_sem.at[0])
    tok_load.start()

    barrier = pltpu.get_barrier_semaphore()

    @pl.loop(0, n - 1)
    def _(k):
        p, e = target(k)
        pl.semaphore_signal(barrier, inc=1, device_id=(p, e), device_id_type=MESH)

    loads = [
        pltpu.make_async_copy(src.at[0], dst, w_sem.at[i])
        for i, (src, dst) in enumerate(((gate_hbm, gate), (up_hbm, up), (down_hbm, down)))
    ]
    for load in loads:
        load.start()

    def outbound(k):
        p, e = target(k)
        return pltpu.make_async_remote_copy(
            src_ref=outgoing.at[k],
            dst_ref=recv.at[k],
            send_sem=send1.at[k],
            recv_sem=recv1.at[k],
            device_id=(p, e),
            device_id_type=MESH,
        )

    def inbound(k):
        p, e = origin(k)
        return pltpu.make_async_remote_copy(
            src_ref=result.at[k],
            dst_ref=returned.at[k],
            send_sem=send2.at[k],
            recv_sem=recv2.at[k],
            device_id=(p, e),
            device_id_type=MESH,
        )

    def row_ids(first, shape, axis):
        at = lax.broadcasted_iota(jnp.int32, shape, axis)
        base = jnp.zeros(shape, jnp.int32)
        for i in range(GROUP):
            p, e = target(first + i)
            base = jnp.where(at // TILE == i, (p * eps + e) * TILE, base)
        return base + at % TILE

    def one_hot(mask):
        return mask.astype(jnp.float32).astype(bf16)

    def pack(first):
        ids = row_ids(first, (rows, tok_rows), 0)
        main = one_hot(row_keys[0:1, :] == ids)
        for j in range(parts):
            cols = pl.ds(j * tail, tail)
            ends = one_hot(row_keys[j + 1:j + 2, :] == ids)
            piece = dot(main, tok[:, cols]) + dot(ends, tok[:, width:])
            outgoing[pl.ds(first, GROUP), :, cols] = piece.astype(bf16).reshape(GROUP, TILE, tail)

    def unpack(first, start):
        ids = row_ids(first, (tok_rows, rows), 1)
        main = one_hot(col_keys[:, 0:1] == ids)
        ends = jnp.zeros((tok_rows, tail), jnp.float32)
        for j in range(parts):
            cols = pl.ds(j * tail, tail)
            piece = returned[pl.ds(first, GROUP), :, cols].reshape(rows, tail)
            head = dot(main, piece).astype(bf16)
            mixed_ref[:, cols] = head if start else mixed_ref[:, cols] + head
            ends = ends + dot(one_hot(col_keys[:, j + 1:j + 2] == ids), piece)
        ends = ends.astype(bf16)
        mixed_ref[:, width:] = ends if start else mixed_ref[:, width:] + ends

    def send(first):
        @pl.loop(0, GROUP)
        def _(i):
            @pl.when(first + i < n - 1)
            def _():
                outbound(first + i).start()

    tok_load.wait()
    pack(0)
    pl.semaphore_wait(barrier, n - 1)
    send(0)

    @pl.loop(1, n // GROUP)
    def _(g):
        pack(g * GROUP)
        send(g * GROUP)

    own = pltpu.make_async_copy(outgoing.at[n - 1], recv.at[n - 1], local_sem.at[0])
    own.start()
    for load in loads:
        load.wait()
    own.wait()

    r = lax.broadcasted_iota(jnp.int32, (rows, rows), 0)
    c = lax.broadcasted_iota(jnp.int32, (rows, rows), 1)
    same = (r // TILE) == (c // TILE)
    r, c = r % TILE, c % TILE

    def spreader(j):
        return one_hot(same & (r // spare == j) & (c == cap + r % spare))

    def folder(j):
        return one_hot(same & (r >= cap) & (c == spare * j + r - cap))

    body_row = (lax.broadcasted_iota(jnp.int32, (rows, 1), 0) % TILE) < cap
    step = 256

    @pl.loop(0, n // GROUP)
    def _(g):
        first = g * GROUP

        @pl.loop(0, GROUP)
        def _(i):
            @pl.when(first + i < n - 1)
            def _():
                outbound(first + i).wait_recv()

        block = recv.at[pl.ds(first, GROUP)]
        total = jnp.zeros((rows, tail), jnp.float32)
        for j in range(parts):
            piece = block[:, :, j * tail:(j + 1) * tail].reshape(rows, tail)
            total = total + dot(spreader(j), piece)
        rest[...] = total.astype(bf16)

        @pl.loop(0, hidden.shape[1] // step)
        def _(f):
            cols = pl.ds(pl.multiple_of(f * step, step), step)
            main = block[...].reshape(rows, width)
            g_out = dot(main, gate[:width, cols]) + dot(rest[...], gate[width:, cols])
            u_out = dot(main, up[:width, cols]) + dot(rest[...], up[width:, cols])
            hidden[:, cols] = (jax.nn.silu(g_out) * u_out).astype(bf16)

        rest[...] = dot(hidden[...], down[:, width:]).astype(bf16)
        for j in range(parts):
            cols = pl.ds(j * tail, tail)
            body = dot(hidden[...], down[:, cols])
            extra = dot(folder(j), rest[...])
            packed = jnp.where(body_row, body, extra).astype(bf16)
            result[pl.ds(first, GROUP), :, cols] = packed.reshape(GROUP, TILE, tail)

        @pl.loop(0, GROUP)
        def _(i):
            @pl.when(first + i < n - 1)
            def _():
                inbound(first + i).start()

    mine = pltpu.make_async_copy(result.at[n - 1], returned.at[n - 1], local_sem.at[1])
    mine.start()
    mine.wait()

    def collect(first):
        @pl.loop(0, GROUP)
        def _(i):
            @pl.when(first + i < n - 1)
            def _():
                inbound(first + i).wait_recv()

    collect(0)
    unpack(0, True)

    @pl.loop(1, n // GROUP)
    def _(g):
        collect(g * GROUP)
        unpack(g * GROUP, False)

    @pl.loop(0, n - 1)
    def _(k):
        outbound(k).wait_send()
        inbound(k).wait_send()


def fused(tokens, routed, slot, w_gate, w_up, w_down, pairs, eps, cap):
    n = pairs * eps
    tok_rows, depth = tokens.shape
    ff = w_gate.shape[2]
    spare = TILE - cap
    parts = cap // spare
    tail = depth * spare // TILE
    width = depth - tail

    rest_key = jnp.where(
        slot[None, :] // spare == jnp.arange(parts)[:, None],
        (routed * TILE + cap + slot % spare)[None, :],
        -1,
    )
    keys = jnp.concatenate([(routed * TILE + slot)[None, :], rest_key], axis=0)

    vmem = pl.BlockSpec(memory_space=pltpu.VMEM)
    hbm = pl.BlockSpec(memory_space=pl.ANY)
    bf16 = jnp.bfloat16
    parcels = pltpu.VMEM((n, TILE, width), bf16)
    return pl.pallas_call(
        functools.partial(exchange_ffn, pairs, eps, cap),
        out_shape=jax.ShapeDtypeStruct((tok_rows, depth), bf16),
        in_specs=[vmem, vmem, hbm, hbm, hbm, hbm],
        out_specs=vmem,
        scratch_shapes=[
            pltpu.VMEM((tok_rows, depth), bf16),
            parcels,
            parcels,
            parcels,
            parcels,
            pltpu.VMEM((depth, ff), bf16),
            pltpu.VMEM((depth, ff), bf16),
            pltpu.VMEM((ff, depth), bf16),
            pltpu.VMEM((GROUP * TILE, ff), bf16),
            pltpu.VMEM((GROUP * TILE, tail), bf16),
            pltpu.SemaphoreType.DMA((1,)),
            pltpu.SemaphoreType.DMA((3,)),
            pltpu.SemaphoreType.DMA((2,)),
            pltpu.SemaphoreType.DMA((n,)),
            pltpu.SemaphoreType.DMA((n,)),
            pltpu.SemaphoreType.DMA((n,)),
            pltpu.SemaphoreType.DMA((n,)),
        ],
        compiler_params=pltpu.CompilerParams(
            collective_id=0, has_side_effects=True, vmem_limit_bytes=56 * 1024 * 1024
        ),
        name="exchange_ffn",
    )(keys, keys.T, tokens, w_gate, w_up, w_down)


def plain(tokens, routed, slot, w_gate, w_up, w_down, experts, capacity):
    position = routed * capacity + slot
    outgoing = (
        jnp.zeros((experts * capacity, tokens.shape[1]), jnp.bfloat16).at[position].set(tokens)
    )
    parcel = lax.all_to_all(
        outgoing.reshape(experts, capacity, outgoing.shape[1]),
        ("pair", "ep"), split_axis=0, concat_axis=0, tiled=True,
    )
    flat_rows = parcel.reshape(experts * capacity, parcel.shape[2])
    gate_proj = dot(flat_rows, w_gate[0])
    up_proj = dot(flat_rows, w_up[0])
    hidden = (jax.nn.silu(gate_proj) * up_proj).astype(jnp.bfloat16)
    result = dot(hidden, w_down[0]).astype(jnp.bfloat16)
    returned = lax.all_to_all(
        result.reshape(experts, capacity, result.shape[1]),
        ("pair", "ep"), split_axis=0, concat_axis=0, tiled=True,
    )
    return jnp.take(returned.reshape(experts * capacity, -1), position, axis=0)


def shards(tokens, expert_of, w_gate, w_up, w_down):
    pairs = lax.axis_size("pair")
    eps = lax.axis_size("ep")
    experts = pairs * eps
    tok_rows, depth = tokens.shape
    cap = tok_rows // experts + tok_rows // (2 * experts)
    routed = expert_of[:, 0]
    onehot = (routed[:, None] == jnp.arange(experts, dtype=jnp.int32)[None, :]).astype(jnp.float32)
    order = jnp.arange(tok_rows)
    earlier = (order[:, None] > order[None, :]).astype(jnp.bfloat16)
    before = dot(earlier, onehot.astype(jnp.bfloat16))
    slot = jnp.sum(before * onehot, axis=1).astype(jnp.int32)
    spare = TILE - cap
    packs = 0 < spare <= cap and cap % spare == 0 and (depth * spare) % (TILE * 256) == 0
    if packs and experts % GROUP == 0 and w_gate.shape[2] % 256 == 0:
        return fused(tokens, routed, slot, w_gate, w_up, w_down, pairs, eps, cap)
    return plain(tokens, routed, slot, w_gate, w_up, w_down, experts, cap)


def solution(mesh):
    spec2 = P(("pair", "ep"), None)
    spec3 = P(("pair", "ep"), None, None)
    return jax.shard_map(
        shards,
        mesh=mesh,
        in_specs=(spec2, spec2, spec3, spec3, spec3),
        out_specs=spec2,
        check_vma=False,
    )
```

time: 165 us -> 160 us (0.970)
  matrix products: 8.25 us -> 0.95 us
  other arithmetic: 4.35 us -> 1.4 us
  local copies, waits for them, and re-layouts: 1.75 us -> 3.93 us
  Pallas kernels: 151 us -> 153 us
    dot_general x5 -> x1, matrix products: 6.06 us -> 0.95 us  [dot(): return jnp.dot(a, b, preferred_element_type=jnp.float32)]
    concatenate x2 -> x1, other arithmetic: 3.27 us -> 0.01 us  [fused(): keys = jnp.concatenate([(routed * TILE + slot)[None, :], rest_key], axis=0)]
    unnamed x2 -> x3, local copies, waits for them, and re-layouts: 0.01 us -> 3.13 us
    pallas_call x1, Pallas kernels: 151 us -> 153 us  [fused(): pl.pallas_call(functools.partial(exchange_ffn, pairs, eps, cap), out_shap...]
    dot_general x3 -> x0, matrix products: 2.18 us -> none  [fused(): lax.dot_general(both, rows, (((0,), (0,)), ((), ())), preferred_element_t...]
    slice x2 -> x0, local copies, waits for them, and re-layouts: 1.75 us -> none  [the longest x1 1.74 us: fused(): rows = jnp.concatenate([tokens[:, j * tail:(j + 1) * tail], last], axis=0)]
where the time goes in v2:
time: 160 us; the launch traced here: 159 us
  Pallas kernels  153 us (96%)
  local copies, waits for them, and re-layouts  3.93 us (2%)
    pallas_call x1, Pallas kernels, fused(): pl.pallas_call(functools.partial(exchange_ffn, pairs, eps, cap), out_shap...  153 us

profile of v2, /device:TPU:12, one launch (start us, length us, event | category | flops | bytes accessed | tf_op | source)
XLA Modules:
  0.0 159.4 jit_solution(1721939921381119299)
XLA Ops:
  0.0 1.0 fusion
  1.0 0.7 bitcast_add_fusion
  1.7 0.7 and_select_fusion.1
  2.4 0.0 copy-start
  2.4 0.8 copy.10
  3.2 0.0 copy-done
  3.2 153.1 %exchange_ffn.1 = bf16[256,4096]{1,0:T(8,128)(2,1)} custom-call(s32[4,256]{1,0:T(4,128)} %copy-done, s32[256,4]{1,0:T(8,128)} %bitcast.5, bf16[256,4096]{1,0:T(8,128)(2,1)} %tok_hbm.1, bf16[1,4096,768]{2,1,0:T(8,128)(2,1)} %gate_hbm.1, bf16[1,4096,768]{2,1,0:T(8,128)(2,1)} %up_hbm.1, bf16[1,768,4096]{2,1,0:T(8,128)(2,1)} %down_hbm.1), custom_call_target="tpu_custom_call" | custom-call | tf_op jit(solution)/shard_map/exchange_ffn/pallas_call | solution.py:240
  156.3 3.1 %copy.12 = bf16[256,4096]{1,0:T(8,128)(2,1)} copy(bf16[256,4096]{1,0:T(8,128)(2,1)} %exchange_ffn.1) | data formatting | bytes 4194304
  (3 shorter events, 0.0 us)
Async XLA Ops:
  2.4 0.8 copy-start

commit v3 on v2

--- a/solution.py
+++ b/solution.py
@@ -17,7 +17,7 @@
 
 
 def exchange_ffn(
-    pairs, eps, cap, row_keys, col_keys, tok_hbm, gate_hbm, up_hbm, down_hbm, mixed_ref,
+    pairs, eps, cap, row_keys, col_keys, tok_hbm, gate_hbm, up_hbm, down_hbm, head_ref, ends_ref,
     tok, outgoing, recv, result, returned, gate, up, down, hidden, rest,
     tok_sem, w_sem, local_sem, send1, recv1, send2, recv2,
 ):
@@ -111,10 +111,10 @@
             cols = pl.ds(j * tail, tail)
             piece = returned[pl.ds(first, GROUP), :, cols].reshape(rows, tail)
             head = dot(main, piece).astype(bf16)
-            mixed_ref[:, cols] = head if start else mixed_ref[:, cols] + head
+            head_ref[:, cols] = head if start else head_ref[:, cols] + head
             ends = ends + dot(one_hot(col_keys[:, j + 1:j + 2] == ids), piece)
         ends = ends.astype(bf16)
-        mixed_ref[:, width:] = ends if start else mixed_ref[:, width:] + ends
+        ends_ref[...] = ends if start else ends_ref[...] + ends
 
     def send(first):
         @pl.loop(0, GROUP)
@@ -237,11 +237,14 @@
     hbm = pl.BlockSpec(memory_space=pl.ANY)
     bf16 = jnp.bfloat16
     parcels = pltpu.VMEM((n, TILE, width), bf16)
-    return pl.pallas_call(
+    head, ends = pl.pallas_call(
         functools.partial(exchange_ffn, pairs, eps, cap),
-        out_shape=jax.ShapeDtypeStruct((tok_rows, depth), bf16),
+        out_shape=[
+            jax.ShapeDtypeStruct((tok_rows, width), bf16),
+            jax.ShapeDtypeStruct((tok_rows, tail), bf16),
+        ],
         in_specs=[vmem, vmem, hbm, hbm, hbm, hbm],
-        out_specs=vmem,
+        out_specs=[vmem, vmem],
         scratch_shapes=[
             pltpu.VMEM((tok_rows, depth), bf16),
             parcels,
@@ -266,6 +269,7 @@
         ),
         name="exchange_ffn",
     )(keys, keys.T, tokens, w_gate, w_up, w_down)
+    return jnp.concatenate([head, ends], axis=1)
 
 
 def plain(tokens, routed, slot, w_gate, w_up, w_down, experts, capacity):

time: 160 us -> 160 us (level)
  local copies, waits for them, and re-layouts: 3.93 us -> 0.81 us
  other arithmetic: 1.4 us -> 4.48 us
    unnamed x3 -> x2, local copies, waits for them, and re-layouts: 3.13 us -> 0.01 us
    concatenate x0 -> x1, other arithmetic: none -> 3.08 us  [fused(): return jnp.concatenate([head, ends], axis=1)]
where the time goes in v3:
time: 160 us; the launch traced here: 159 us
  Pallas kernels  153 us (96%)
  other arithmetic  4.48 us (3%)
    pallas_call x1, Pallas kernels, fused(): pl.pallas_call(functools.partial(exchange_ffn, pairs, eps, cap), out_shap...  153 us

profile of v3, /device:TPU:12, one launch (start us, length us, event | category | flops | bytes accessed | tf_op | source)
XLA Modules:
  0.0 159.3 jit_solution(7596673411855083095)
XLA Ops:
  0.0 1.0 fusion
  1.0 0.7 bitcast_add_fusion
  1.7 0.7 and_select_fusion.1
  2.4 0.0 copy-start
  2.4 0.8 copy.10
  3.2 0.0 copy-done
  3.2 153.1 %exchange_ffn.1 = (bf16[256,3072]{1,0:T(8,128)(2,1)}, bf16[256,1024]{1,0:T(8,128)(2,1)}) custom-call(s32[4,256]{1,0:T(4,128)} %copy-done, s32[256,4]{1,0:T(8,128)} %bitcast.5, bf16[256,4096]{1,0:T(8,128)(2,1)} %tok_hbm.1, bf16[1,4096,768]{2,1,0:T(8,128)(2,1)} %gate_hbm.1, bf16[1,4096,768]{2,1,0:T(8,128)(2,1)} %up_hbm.1, bf16[1,768,4096]{2,1,0:T(8,128)(2,1)} %down_hbm.1), custom_call_target="tpu_custom_call" | custom-call | tf_op jit(solution)/shard_map/exchange_ffn/pallas_call | solution.py:240
  156.3 3.1 %pad_maximum_fusion = bf16[256,4096]{1,0:T(8,128)(2,1)} fusion(bf16[256,1024]{1,0:T(8,128)(2,1)} %get-tuple-element.8, bf16[256,3072]{1,0:T(8,128)(2,1)} %get-tuple-element.7), kind=kLoop, calls=%fused_computation | loop fusion | flops 4194304 | bytes 4194304 | tf_op jit(solution)/shard_map/concatenate | solution.py:272
  (3 shorter events, 0.0 us)
Async XLA Ops:
  2.4 0.8 copy-start
